TPU v7x, 32 devices: a whole 2x2x4 slice. The times are simulated.
32 devices in a mesh: tm: 4 (over y, x), space: 8 (over z, core).
Axes of the slice: x: 2, y: 2, z: 4, core: 2. Of those that a mesh axis runs over, the one named last changes fastest.
Arguments:
- fields: bfloat16 [4096, 2, 16384], P('tm', None, 'space')
- calendar_day: int32 [4096], P('tm'), may hold values from 0 to 364, as said below
- events: int32 [16, 96], replicated, may hold values from 0 to 4080, as said below
- lag_offsets: int32 [16], replicated, may hold values from 0 to 15, each once
Outputs:
- composite: float32 [16, 16, 2, 16384], P('tm', None, None, 'space')
Inputs may be any that keep to these rules, and one draw needn't show every extreme that they name: `calendar_day`: days of the year of successive record days, one or two calendar days apart. `events`: each entry is a record day; a day may repeat within a type. `lag_offsets`: each of 0 to 15 once.
All inputs are finite; a program needn't handle non-finite values.
Results may differ from a plain program's by a relative error of at most 0.0012.
Values may be sent and summed in bfloat16 or wider, within the bound.
A program may use at most 64 MiB of HBM per device.

v0:
```python
import functools

import jax
import jax.numpy as jnp
from jax import lax
from jax.experimental import pallas as pl
from jax.experimental.pallas import tpu as pltpu
from jax.sharding import PartitionSpec as P

HARMONICS = 4
TERMS = 2 * HARMONICS + 1
TWO_PI = 6.283185307179586
PAD = 128
CHUNK = 256
NT = (((1,), (1,)), ((), ()))
TN = (((0,), (0,)), ((), ()))


def regressor_rows(calendar_day):
    phases = jnp.repeat(calendar_day, 2).astype(jnp.float32) * (TWO_PI / 365.25)
    line = lax.iota(jnp.int32, 16)[:, None]
    angles = ((line + 1) // 2).astype(jnp.float32) * phases[None, :]
    rows = jnp.where(line % 2 == 1, jnp.cos(angles), jnp.sin(angles))
    rows = jnp.where(line == 0, 1.0, jnp.where(line < TERMS, rows, 0.0))
    return rows.astype(jnp.bfloat16)


def prepare(days_ref, design_ref, weights_ref, normal_ref):
    members, types = days_ref.shape
    depth = design_ref.shape[1]
    shifts = (weights_ref.shape[0] - 32) // types
    places = lax.broadcasted_iota(jnp.int32, (members, depth + PAD), 1) - PAD
    for kind in range(types):
        hits = (days_ref[:, kind : kind + 1] == places).astype(jnp.float32)
        histogram = jnp.sum(hits, axis=0, keepdims=True)
        wide = jnp.broadcast_to(histogram, (shifts, depth + PAD))
        rolled = pltpu.roll(wide, 0, 1, stride=1, stride_axis=0)
        weights_ref[kind * shifts : (kind + 1) * shifts, :] = rolled[:, PAD:].astype(jnp.bfloat16)
    design = design_ref[...]
    odd = lax.broadcasted_iota(jnp.int32, design.shape, 1) % 2
    wide_design = design.astype(jnp.float32)
    weights_ref[types * shifts : types * shifts + 16, :] = jnp.where(odd == 0, wide_design, 0.0).astype(jnp.bfloat16)
    weights_ref[types * shifts + 16 :, :] = jnp.where(odd == 1, wide_design, 0.0).astype(jnp.bfloat16)
    normal_ref[...] = lax.dot_general(design, weights_ref[...], NT, preferred_element_type=jnp.float32)


def split3(value):
    high = value.astype(jnp.bfloat16)
    rest = value - high.astype(jnp.float32)
    middle = rest.astype(jnp.bfloat16)
    low = (rest - middle.astype(jnp.float32)).astype(jnp.bfloat16)
    return high, middle, low


def encode(part):
    top = jnp.max(jnp.abs(part), axis=0, keepdims=True)
    factor = jnp.where(top > 0.0, 32767.0 / jnp.where(top > 0.0, top, 1.0), 0.0)
    return jnp.round(part * factor).astype(jnp.int32).astype(jnp.int16), top * (1.0 / 32767.0)


def decode(codes, scale):
    return codes.astype(jnp.int32).astype(jnp.float32) * scale


def flip(index, bits):
    bit = 1
    flipped = index
    while bit <= bits:
        if bits & bit:
            flipped = flipped + bit - 2 * bit * lax.rem(lax.div(index, bit), 2)
        bit *= 2
    return flipped


def compose(
    tm, space, members, all_points,
    fields, weights_hbm, normal_ref, out_ref, mean_ref,
    xs, weights_ref, normals, left, whole, parts, codes, scales, got_codes, got_scales, sums, got_sums,
    w_sem, x_sems, n_send, n_recv, c_send, c_recv, s_send, s_recv, m_send, m_recv,
):
    chunks, rows, _ = out_ref.shape
    count_rows = weights_ref.shape[0] - 32
    me = lax.axis_index("tm")
    here = lax.axis_index("space")
    stages = tm.bit_length() - 1

    def load(c):
        return pltpu.make_async_copy(
            fields.at[:, :, pl.ds(pl.multiple_of(c * CHUNK, CHUNK), CHUNK)], xs.at[c], x_sems.at[c]
        )

    load_weights = pltpu.make_async_copy(weights_hbm, weights_ref, w_sem)
    load_weights.start()
    lax.fori_loop(0, chunks, lambda c, _: (load(c).start(), 0)[1], 0)

    barrier = pltpu.get_barrier_semaphore()
    for i in range(1, tm):
        pl.semaphore_signal(barrier, inc=1, device_id={"tm": lax.rem(me + i, tm)})
    for i in range(1, space):
        pl.semaphore_signal(barrier, inc=1, device_id={"space": lax.rem(here + i, space)})
    pl.semaphore_wait(barrier, tm + space - 2)

    def send_normal(i):
        return pltpu.make_async_remote_copy(
            normal_ref, normals.at[i - 1], n_send.at[i - 1], n_recv.at[i - 1], device_id={"tm": lax.rem(me + i, tm)}
        )

    def send_code(apart, bit, c):
        peer = {"tm": flip(me, bit)}
        d = apart - 1
        return (
            pltpu.make_async_remote_copy(
                codes.at[d, c], got_codes.at[d, c], c_send.at[d, c], c_recv.at[d, c], device_id=peer
            ),
            pltpu.make_async_remote_copy(
                scales.at[d, c], got_scales.at[d, c], s_send.at[d, c], s_recv.at[d, c], device_id=peer
            ),
        )

    def send_sums(i):
        return pltpu.make_async_remote_copy(
            sums, got_sums.at[i - 1], m_send.at[i - 1], m_recv.at[i - 1],
            device_id={"space": lax.rem(here + i, space)},
        )

    for i in range(1, tm):
        send_normal(i).start()
    system = normal_ref[...]
    for i in range(1, tm):
        send_normal(i).wait()
        system = system + normals[i - 1]
    lines = lax.broadcasted_iota(jnp.int32, system.shape, 0)
    for k in range(TERMS):
        pivot = system[k : k + 1, :] / system[k : k + 1, count_rows + k : count_rows + k + 1]
        system = jnp.where(lines == k, pivot, system - system[:, count_rows + k : count_rows + k + 1] * pivot)
    fit = system[:, :count_rows]
    fit = jnp.where(lax.broadcasted_iota(jnp.int32, fit.shape, 0) < TERMS, fit, 0.0)
    odd = lax.broadcasted_iota(jnp.int32, fit.shape, 1) % 2
    fit = jnp.concatenate([jnp.where(odd == 0, fit, 0.0), jnp.where(odd == 1, fit, 0.0)], axis=0)
    high, middle, low = split3(fit)
    left[...] = jnp.concatenate([high, high, high, middle, middle, low], axis=0)
    load_weights.wait()

    def bits_of(turn):
        return [1 << ((turn + stage) % stages) for stage in range(stages)]

    def leaving(turn, stage):
        bits = bits_of(turn)
        return [
            apart for apart in range(1, tm)
            if apart & bits[stage] and not any(apart & bit for bit in bits[:stage])
        ]

    def each_chunk(body, start):
        def group(g, carry):
            for turn in range(stages):
                carry = body(g * stages + turn, turn, carry)
            return carry

        return lax.fori_loop(0, chunks // stages, group, start)

    def post(c, turn, stage):
        for apart in leaving(turn, stage):
            codes[apart - 1, c], scales[apart - 1, c] = encode(parts[apart, c])
            for copy in send_code(apart, bits_of(turn)[stage], c):
                copy.start()

    def collect(c, turn, stage):
        bit = bits_of(turn)[stage]
        for apart in leaving(turn, stage):
            for copy in send_code(apart, bit, c):
                copy.wait()
            parts[apart - bit, c] += decode(got_codes[apart - 1, c], got_scales[apart - 1, c])

    def compute(c, turn, carry):
        load(c).wait()
        block = xs[c].reshape(weights_ref.shape[1], CHUNK)
        raw = jnp.dot(weights_ref[...], block, preferred_element_type=jnp.float32)
        p_high, p_middle, p_low = split3(raw[count_rows:])
        right = jnp.concatenate([p_high, p_middle, p_low, p_high, p_middle, p_high], axis=0)
        whole[...] = raw[:count_rows] - lax.dot_general(left[...], right, TN, preferred_element_type=jnp.float32)
        for apart in range(tm):
            parts[apart, c] = whole[pl.ds(pl.multiple_of(flip(me, apart) * rows, rows), rows), :]
        post(c, turn, 0)
        return carry

    each_chunk(compute, 0)

    for stage in range(1, stages):
        def relay(c, turn, carry):
            collect(c, turn, stage - 1)
            post(c, turn, stage)
            return carry

        each_chunk(relay, 0)

    ones = jnp.ones((8, CHUNK), jnp.bfloat16)

    def gather(c, turn, total):
        collect(c, turn, stages - 1)
        value = parts[0, c] * (1.0 / members)
        out_ref[c] = value
        for piece in split3(value):
            total = total + lax.dot_general(ones, piece, NT, preferred_element_type=jnp.float32)
        return total

    sums[...] = each_chunk(gather, jnp.zeros((8, rows), jnp.float32))
    for i in range(1, space):
        send_sums(i).start()
    total = sums[...]
    for i in range(1, space):
        send_sums(i).wait()
        total = total + got_sums[i - 1]
    mean_ref[...] = lax.dot_general(
        total * (1.0 / (8 * all_points)), jnp.ones((8, CHUNK), jnp.float32), TN,
        precision=lax.Precision.HIGHEST, preferred_element_type=jnp.float32,
    )


def finish(lags_ref, values_ref, mean_ref, out_ref, natural):
    chunks = values_ref.shape[0]
    lag_count = out_ref.shape[1]
    mean = mean_ref[...]
    for c in range(chunks):
        centred = values_ref[c] - mean
        natural[:, :, c * CHUNK : (c + 1) * CHUNK] = centred.reshape(lag_count, 2, CHUNK)
    for lag in range(lag_count):
        out_ref[0, lag] = natural[lags_ref[lag]]


def shards(tm, space, fields, calendar_day, events, lag_offsets):
    types, members = events.shape
    lag_count = lag_offsets.shape[0]
    days, variables, points = fields.shape
    depth = variables * days
    count_rows = types * lag_count * variables
    rows = count_rows // tm
    chunks = points // CHUNK
    places = 2 * (events - lax.axis_index("tm") * days).T
    weights, normal = pl.pallas_call(
        prepare,
        out_shape=(
            jax.ShapeDtypeStruct((count_rows + 32, depth), jnp.bfloat16),
            jax.ShapeDtypeStruct((16, count_rows + 32), jnp.float32),
        ),
        in_specs=[pl.BlockSpec(memory_space=pltpu.VMEM)] * 2,
        out_specs=[pl.BlockSpec(memory_space=pltpu.VMEM)] * 2,
        compiler_params=pltpu.CompilerParams(vmem_limit_bytes=48 * 2**20),
        name="prepare",
    )(places, regressor_rows(calendar_day))
    pairs = (tm - 1, chunks)
    dma = pltpu.SemaphoreType.DMA
    values, mean = pl.pallas_call(
        functools.partial(compose, tm, space, members, points * space),
        out_shape=(
            jax.ShapeDtypeStruct((chunks, rows, CHUNK), jnp.float32),
            jax.ShapeDtypeStruct((rows, CHUNK), jnp.float32),
        ),
        in_specs=[
            pl.BlockSpec(memory_space=pl.ANY),
            pl.BlockSpec(memory_space=pl.ANY),
            pl.BlockSpec(memory_space=pltpu.VMEM),
        ],
        out_specs=[pl.BlockSpec(memory_space=pltpu.VMEM)] * 2,
        scratch_shapes=[
            pltpu.VMEM((chunks, days, variables, CHUNK), jnp.bfloat16),
            pltpu.VMEM((count_rows + 32, depth), jnp.bfloat16),
            pltpu.VMEM((tm - 1, 16, count_rows + 32), jnp.float32),
            pltpu.VMEM((192, count_rows), jnp.bfloat16),
            pltpu.VMEM((count_rows, CHUNK), jnp.float32),
            pltpu.VMEM((tm, chunks, rows, CHUNK), jnp.float32),
            pltpu.VMEM(pairs + (rows, CHUNK), jnp.int16),
            pltpu.VMEM(pairs + (1, CHUNK), jnp.float32),
            pltpu.VMEM(pairs + (rows, CHUNK), jnp.int16),
            pltpu.VMEM(pairs + (1, CHUNK), jnp.float32),
            pltpu.VMEM((8, rows), jnp.float32),
            pltpu.VMEM((space - 1, 8, rows), jnp.float32),
            dma, dma((chunks,)),
            dma((tm - 1,)), dma((tm - 1,)),
            dma(pairs), dma(pairs), dma(pairs), dma(pairs),
            dma((space - 1,)), dma((space - 1,)),
        ],
        compiler_params=pltpu.CompilerParams(
            collective_id=0, has_side_effects=True, vmem_limit_bytes=48 * 2**20
        ),
        name="compose",
    )(fields, weights, normal)
    shifts = lag_count * variables
    return pl.pallas_call(
        finish,
        grid=(types // tm,),
        out_shape=jax.ShapeDtypeStruct((types // tm, lag_count, variables, points), jnp.float32),
        in_specs=[
            pl.BlockSpec(memory_space=pltpu.SMEM),
            pl.BlockSpec((chunks, shifts, CHUNK), lambda kind: (0, kind, 0)),
            pl.BlockSpec((shifts, CHUNK), lambda kind: (kind, 0)),
        ],
        out_specs=pl.BlockSpec((1, lag_count, variables, points), lambda kind: (kind, 0, 0, 0)),
        scratch_shapes=[pltpu.VMEM((lag_count, variables, points), jnp.float32)],
        compiler_params=pltpu.CompilerParams(vmem_limit_bytes=40 * 2**20),
        name="finish",
    )(lag_offsets, values, mean)


def solution(mesh):
    return jax.shard_map(
        functools.partial(shards, mesh.shape["tm"], mesh.shape["space"]),
        mesh=mesh,
        in_specs=(P("tm", None, "space"), P("tm"), P(), P()),
        out_specs=P("tm", None, None, "space"),
        check_vma=False,
    )
```

profile of v0, /device:TPU:0, one launch (start us, length us, event | category | flops | bytes accessed | tf_op | source)
XLA Modules:
  0.0 46.7 jit_solution(2727560769243494252)
XLA Ops:
  0.0 0.0 copy-start
  0.0 0.7 %convert_multiply_fusion = f32[1024]{0:T(1024)S(1)} fusion(s32[1024]{0:T(1024)} %param.5), kind=kLoop, calls=%fused_computation.7 | loop fusion | flops 2048 | bytes 8192 | tf_op jit(solution)/shard_map/mul | solution.py:20
  0.7 0.7 %subtract_multiply_fusion = s32[16,96]{1,0:T(8,128)S(1)} fusion(s32[16,96]{1,0:T(8,128)} %param.6, s32[]{:T(128)S(6)} %mul.38), kind=kLoop, calls=%fused_computation.6 | loop fusion | flops 3072 | bytes 12292 | tf_op jit(solution)/shard_map/mul | solution.py:239
  1.4 0.1 copy.11
  1.5 0.2 broadcast_in_dim.41
  1.7 0.3 mul.45
  2.0 0.6 %fusion.3.design_ref = bf16[16,2048]{1,0:T(8,128)(2,1)S(1)} fusion(f32[2048]{0:T(1024)S(1)} %mul.45, f32[16]{0:T(128)S(1)} %fusion.5, pred[16]{0:T(512)(128)(4,1)S(1)} %get-tuple-element.13, pred[16]{0:T(512)(128)(4,1)S(1)} %get-tuple-element.14, pred[16]{0:T(512)(128)(4,1)S(1)} %iota_compare_fusion.1), kind=kLoop, calls=%fused_computation.5 | loop fusion | flops 163840 | bytes 73840 | tf_op jit(solution)/shard_map/convert_element_type | solution.py:25
  2.5 3.0 %prepare.1 = (bf16[544,2048]{1,0:T(8,128)(2,1)S(1)}, f32[16,544]{1,0:T(8,128)S(1)}) custom-call(s32[96,16]{1,0:T(8,128)S(1)} %bitcast.1, bf16[16,2048]{1,0:T(8,128)(2,1)S(1)} %fusion.3.design_ref), custom_call_target="tpu_custom_call" | custom-call | tf_op jit(solution)/shard_map/prepare/pallas_call | solution.py:240
  5.5 38.8 %compose.1 = (f32[8,128,256]{2,1,0:T(8,128)S(1)}, f32[128,256]{1,0:T(8,128)S(1)}) custom-call(bf16[1024,2,2048]{2,1,0:T(2,128)(2,1)} %fields.1, bf16[544,2048]{1,0:T(8,128)(2,1)S(1)} %get-tuple-element.9.weights_hbm, f32[16,544]{1,0:T(8,128)S(1)} %get-tuple-element.10.normal_ref), custom_call_target="tpu_custom_call" | custom-call | tf_op jit(solution)/shard_map/compose/pallas_call | solution.py:253
  44.3 0.0 copy-done
  44.4 2.3 %finish.1 = f32[4,16,2,2048]{3,2,1,0:T(2,128)} custom-call(s32[16]{0:T(128)S(1)} %copy-done, f32[8,128,256]{2,1,0:T(8,128)S(1)} %get-tuple-element.11.values_ref, f32[128,256]{1,0:T(8,128)S(1)} %get-tuple-element.12.mean_ref), custom_call_target="tpu_custom_call" | custom-call | tf_op jit(solution)/shard_map/finish/pallas_call | solution.py:289
  (3 shorter events, 0.0 us)
Async XLA Ops:
  0.0 44.3 %copy-start = (s32[16]{0:T(128)S(1)}, s32[16]{0:T(128)}, u32[]{:S(2)}) copy-start(s32[16]{0:T(128)} %lags_ref.1) | copy-start | bytes 196
where the time goes:
time: 46.9 us; the launch traced here: 46.7 us
  Pallas kernels  44.1 us (94%)
  other arithmetic  1.96 us (4%)
  local copies, waits for them, and re-layouts  0.56 us (1%)
    pallas_call x1, Pallas kernels, shards(): pl.pallas_call(functools.partial(compose, tm, space, members, points * sp...  38.8 us
    pallas_call x1, Pallas kernels, shards(): pl.pallas_call(prepare, out_shape=(jax.ShapeDtypeStruct((count_rows + 32,...  2.98 us
    pallas_call x1, Pallas kernels, shards(): pl.pallas_call(finish, grid=(types // tm,), out_shape=jax.ShapeDtypeStruc...  2.3 us

commit v1 on v0

v1 whole, which is shorter than its diff:
```python
import functools

import jax
import jax.numpy as jnp
from jax import lax
from jax.experimental import pallas as pl
from jax.experimental.pallas import tpu as pltpu
from jax.sharding import PartitionSpec as P

HARMONICS = 4
TERMS = 2 * HARMONICS + 1
TWO_PI = 6.283185307179586
LANES = 128
PAD = 128
CHUNK = 256
AHEAD = 4
NN = (((1,), (0,)), ((), ()))
NT = (((1,), (1,)), ((), ()))
TN = (((0,), (0,)), ((), ()))


def split3(value):
    high = value.astype(jnp.bfloat16)
    rest = value - high.astype(jnp.float32)
    middle = rest.astype(jnp.bfloat16)
    low = (rest - middle.astype(jnp.float32)).astype(jnp.bfloat16)
    return high, middle, low


def encode(part):
    top = jnp.max(jnp.abs(part), axis=0, keepdims=True)
    factor = jnp.where(top > 0.0, 32767.0 / jnp.where(top > 0.0, top, 1.0), 0.0)
    return jnp.round(part * factor).astype(jnp.int32).astype(jnp.int16), top * (1.0 / 32767.0)


def decode(codes, scale):
    return codes.astype(jnp.int32).astype(jnp.float32) * scale


def flip(index, bits):
    bit = 1
    flipped = index
    while bit <= bits:
        if bits & bit:
            flipped = flipped + bit - 2 * bit * lax.rem(lax.div(index, bit), 2)
        bit *= 2
    return flipped


def ones_where(condition):
    return jnp.where(condition, 1.0, 0.0).astype(jnp.bfloat16)


def count_weights(places, weights_ref, depth):
    types, members = places.shape
    shifts = (weights_ref.shape[0] - 32) // types
    tiles = (depth + PAD) // LANES
    upper = lax.shift_right_arithmetic(places, 7)
    lower = lax.bitwise_and(places, LANES - 1)
    tile_lines = lax.broadcasted_iota(jnp.int32, (-(-tiles // 8) * 8, members), 0)
    lane_lines = lax.broadcasted_iota(jnp.int32, (LANES, members), 0)
    for kind in range(types):
        in_tile = ones_where(upper[kind : kind + 1, :] == tile_lines)
        in_lane = ones_where(lower[kind : kind + 1, :] == lane_lines)
        histogram = lax.dot_general(in_tile, in_lane, NT, preferred_element_type=jnp.float32)
        wide = jnp.concatenate(
            [jnp.broadcast_to(histogram[tile : tile + 1, :], (shifts, LANES)) for tile in range(tiles)], axis=1
        )
        rolled = pltpu.roll(wide, 0, 1, stride=1, stride_axis=0)
        weights_ref[kind * shifts : (kind + 1) * shifts, :] = rolled[:, PAD:].astype(jnp.bfloat16)


def regressors(calendar, weights_ref):
    phase = calendar.astype(jnp.float32) * (TWO_PI / 365.25)
    cosines, sines = [jnp.cos(phase)], [jnp.sin(phase)]
    for order in range(2, HARMONICS + 1):
        a, b = order // 2 - 1, order - order // 2 - 1
        cosines.append(cosines[a] * cosines[b] - sines[a] * sines[b])
        sines.append(sines[a] * cosines[b] + cosines[a] * sines[b])
    terms = [jnp.ones_like(phase)]
    for order in range(HARMONICS):
        terms += [cosines[order], sines[order]]
    tiles = calendar.shape[0]
    line = lax.broadcasted_iota(jnp.int32, (16, LANES), 0)
    blocks = []
    for tile in range(tiles):
        block = jnp.zeros((16, LANES), jnp.float32)
        for term, values in enumerate(terms):
            block = jnp.where(line == term, values[tile : tile + 1, :], block)
        blocks.append(block)
    stacked = jnp.concatenate(blocks, axis=0).astype(jnp.bfloat16)
    day = lax.broadcasted_iota(jnp.int32, (LANES, 2 * LANES), 0)
    place = lax.broadcasted_iota(jnp.int32, (LANES, 2 * LANES), 1)
    first = ones_where(place == 2 * day)
    second = ones_where(place == 2 * day + 1)
    base = weights_ref.shape[0] - 32
    spread = []
    for matrix in (first, second):
        wide = jnp.dot(stacked, matrix, preferred_element_type=jnp.float32)
        spread.append(jnp.concatenate([wide[16 * tile : 16 * tile + 16, :] for tile in range(tiles)], axis=1))
    weights_ref[base : base + 16, :] = spread[0].astype(jnp.bfloat16)
    weights_ref[base + 16 :, :] = spread[1].astype(jnp.bfloat16)
    return (spread[0] + spread[1]).astype(jnp.bfloat16)


def solve(system, count_rows):
    lines = lax.broadcasted_iota(jnp.int32, (16, LANES), 0)
    columns = [
        jnp.broadcast_to(system[:, count_rows + k : count_rows + k + 1], (16, LANES)) for k in range(TERMS)
    ]
    sides = [system[:, start : start + LANES] for start in range(0, count_rows, LANES)]
    for k in range(TERMS):
        column = columns[k]
        inverse = 1.0 / column[k : k + 1, :]

        def eliminate(block):
            pivot = block[k : k + 1, :] * inverse
            return jnp.where(lines == k, pivot, block - column * pivot)

        sides = [eliminate(block) for block in sides]
        columns = [eliminate(block) if j > k else block for j, block in enumerate(columns)]
    return jnp.concatenate([jnp.where(lines < TERMS, block, 0.0) for block in sides], axis=1)


def compose(
    tm, space, members, all_points,
    fields, calendar, events, out_ref,
    xs, calendar_ref, events_ref, weights_ref, normal_ref, normals, left, raws, whole, spatial, parts,
    sums, got_sums, totals, got_totals, means, codes, scales, got_codes, got_scales,
    x_sems, in_sems, n_send, n_recv, m_send, m_recv, t_send, t_recv, c_send, c_recv, s_send, s_recv,
):
    chunks, days = xs.shape[0], xs.shape[1]
    depth = weights_ref.shape[1]
    count_rows = weights_ref.shape[0] - 32
    rows = count_rows // tm
    me = lax.axis_index("tm")
    here = lax.axis_index("space")
    stages = tm.bit_length() - 1

    def load(c):
        return pltpu.make_async_copy(
            fields.at[:, :, pl.ds(pl.multiple_of(c * CHUNK, CHUNK), CHUNK)], xs.at[c], x_sems.at[c]
        )

    barrier = pltpu.get_barrier_semaphore()
    for i in range(1, tm):
        pl.semaphore_signal(barrier, inc=1, device_id={"tm": lax.rem(me + i, tm)})
    for i in range(1, space):
        pl.semaphore_signal(barrier, inc=1, device_id={"space": lax.rem(here + i, space)})
    load_events = pltpu.make_async_copy(events, events_ref, in_sems.at[0])
    load_calendar = pltpu.make_async_copy(calendar, calendar_ref, in_sems.at[1])
    load_events.start()
    load_calendar.start()
    lax.fori_loop(0, chunks, lambda c, _: (load(c).start(), 0)[1], 0)

    def send_normal(i):
        return pltpu.make_async_remote_copy(
            normal_ref, normals.at[i - 1], n_send.at[i - 1], n_recv.at[i - 1], device_id={"tm": lax.rem(me + i, tm)}
        )

    def send_sums(i):
        return pltpu.make_async_remote_copy(
            sums, got_sums.at[i - 1], m_send.at[i - 1], m_recv.at[i - 1],
            device_id={"space": lax.rem(here + i, space)},
        )

    def send_totals(i):
        return pltpu.make_async_remote_copy(
            totals, got_totals.at[i - 1], t_send.at[i - 1], t_recv.at[i - 1],
            device_id={"tm": lax.rem(me + i, tm)},
        )

    def bits_of(turn):
        return [1 << ((turn + stage) % stages) for stage in range(stages)]

    def leaving(turn, stage):
        bits = bits_of(turn)
        return [
            apart for apart in range(1, tm)
            if apart & bits[stage] and not any(apart & bit for bit in bits[:stage])
        ]

    def first_slot(stage):
        return tm - (tm >> stage)

    def send_codes(c, turn, stage):
        peer = {"tm": flip(me, bits_of(turn)[stage])}
        slots = pl.ds(first_slot(stage), tm >> (stage + 1))
        return (
            pltpu.make_async_remote_copy(
                codes.at[c, slots], got_codes.at[c, slots], c_send.at[stage, c], c_recv.at[stage, c], device_id=peer
            ),
            pltpu.make_async_remote_copy(
                scales.at[c, slots], got_scales.at[c, slots], s_send.at[stage, c], s_recv.at[stage, c], device_id=peer
            ),
        )

    load_events.wait()
    count_weights(2 * (events_ref[...] - me * days) + PAD, weights_ref, depth)
    load_calendar.wait()
    design = regressors(calendar_ref[...], weights_ref)
    normal_ref[...] = lax.dot_general(design, weights_ref[...], NT, preferred_element_type=jnp.float32)

    pl.semaphore_wait(barrier, tm + space - 2)
    for i in range(1, tm):
        send_normal(i).start()

    def multiply(c, carry):
        load(c).wait()
        raws[c] = jnp.dot(weights_ref[...], xs[c].reshape(depth, CHUNK), preferred_element_type=jnp.float32)
        return carry

    ahead = -(-AHEAD // stages) * stages
    lax.fori_loop(0, ahead, multiply, 0)

    system = normal_ref[...]
    for i in range(1, tm):
        send_normal(i).wait()
        system = system + normals[i - 1]
    fit = solve(system, count_rows)
    odd = lax.broadcasted_iota(jnp.int32, fit.shape, 1) % 2
    fit = jnp.concatenate([jnp.where(odd == 0, fit, 0.0), jnp.where(odd == 1, fit, 0.0)], axis=0)
    high, middle, low = [piece.astype(jnp.float32) for piece in split3(fit)]
    left[...] = jnp.transpose(jnp.concatenate([high, high, high, middle, middle, low], axis=0)).astype(jnp.bfloat16)
    spatial[...] = jnp.zeros_like(spatial)

    def grouped(body, start, stop):
        def group(g, carry):
            for turn in range(stages):
                body(start + g * stages + turn, turn)
            return carry

        assert (stop - start) % stages == 0
        lax.fori_loop(0, (stop - start) // stages, group, 0)

    def post(c, turn, stage):
        for slot, apart in enumerate(leaving(turn, stage)):
            place = first_slot(stage) + slot
            codes[c, place], scales[c, place] = encode(parts[apart, c])
        for copy in send_codes(c, turn, stage):
            copy.start()

    def collect(c, turn, stage):
        bit = bits_of(turn)[stage]
        for copy in send_codes(c, turn, stage):
            copy.wait_recv()
        for slot, apart in enumerate(leaving(turn, stage)):
            place = first_slot(stage) + slot
            parts[apart - bit, c] += decode(got_codes[c, place], got_scales[c, place])

    def anomalies(c, turn):
        p_high, p_middle, p_low = split3(raws[c, count_rows:, :])
        right = jnp.concatenate([p_high, p_middle, p_low, p_high, p_middle, p_high], axis=0)
        whole[...] = raws[c, :count_rows, :] - jnp.dot(left[...], right, preferred_element_type=jnp.float32)
        for apart in range(tm):
            parts[apart, c] = whole[pl.ds(pl.multiple_of(flip(me, apart) * rows, rows), rows), :]
        post(c, turn, 0)
        spatial[...] += whole[...]

    def both(c, turn):
        anomalies(c, turn)
        multiply(c + ahead, 0)

    grouped(both, 0, chunks - ahead)
    grouped(anomalies, chunks - ahead, chunks)

    ones = jnp.ones((8, CHUNK), jnp.bfloat16)
    total = jnp.zeros((8, count_rows), jnp.float32)
    for piece in split3(spatial[...]):
        total = total + lax.dot_general(ones, piece, NT, preferred_element_type=jnp.float32)
    sums[...] = total[0:1, :]
    for i in range(1, space):
        send_sums(i).start()

    half = chunks // 2

    def relay(stage):
        def body(c, turn):
            collect(c, turn, stage - 1)
            post(c, turn, stage)

        return body

    def spread_sums():
        total = sums[...]
        for i in range(1, space):
            send_sums(i).wait()
            total = total + got_sums[i - 1]
        totals[...] = total
        for i in range(1, tm):
            send_totals(i).start()

    for stage in range(1, stages):
        grouped(relay(stage), 0, half)
        if stage == 1:
            spread_sums()
        grouped(relay(stage), half, chunks)

    total = totals[...]
    for i in range(1, tm):
        send_totals(i).wait()
        total = total + got_totals[i - 1]
    means[...] = lax.dot_general(
        jnp.broadcast_to(total * (1.0 / (8 * members * all_points)), (8, count_rows)), jnp.ones((8, CHUNK), jnp.float32),
        TN, precision=lax.Precision.HIGHEST, preferred_element_type=jnp.float32,
    )

    def gather(c, turn):
        collect(c, turn, stages - 1)
        mean = means[pl.ds(pl.multiple_of(me * rows, rows), rows), :]
        value = parts[0, c] * (1.0 / members) - mean
        out_ref[:, :, :, pl.ds(pl.multiple_of(c * CHUNK, CHUNK), CHUNK)] = value.reshape(out_ref.shape[:3] + (CHUNK,))

    grouped(gather, 0, chunks)

    def sent(c, turn):
        for stage in range(stages):
            for copy in send_codes(c, turn, stage):
                copy.wait_send()

    grouped(sent, 0, chunks)


def finish(lags_ref, natural, out, sems):
    def copy(lag):
        return pltpu.make_async_copy(natural.at[:, lags_ref[lag]], out.at[:, lag], sems.at[lag])

    for lag in range(out.shape[1]):
        copy(lag).start()
    for lag in range(out.shape[1]):
        copy(lag).wait()


def shards(tm, space, fields, calendar_day, events, lag_offsets):
    types, members = events.shape
    lag_count = lag_offsets.shape[0]
    days, variables, points = fields.shape
    depth = variables * days
    count_rows = types * lag_count * variables
    rows = count_rows // tm
    chunks = points // CHUNK
    stages = tm.bit_length() - 1
    dma = pltpu.SemaphoreType.DMA
    vmem = pltpu.VMEM
    f32, bf16 = jnp.float32, jnp.bfloat16
    shape = (types // tm, lag_count, variables, points)
    natural = pl.pallas_call(
        functools.partial(compose, tm, space, members, points * space),
        out_shape=jax.ShapeDtypeStruct(shape, f32),
        in_specs=[pl.BlockSpec(memory_space=pltpu.HBM)] * 3,
        out_specs=pl.BlockSpec(memory_space=vmem),
        scratch_shapes=[
            vmem((chunks, days, variables, CHUNK), bf16),
            vmem((days // LANES, LANES), jnp.int32),
            vmem((types, members), jnp.int32),
            vmem((count_rows + 32, depth), bf16),
            vmem((16, count_rows + 32), f32),
            vmem((tm - 1, 16, count_rows + 32), f32),
            vmem((count_rows, 192), bf16),
            vmem((chunks, count_rows + 32, CHUNK), f32),
            vmem((count_rows, CHUNK), f32),
            vmem((count_rows, CHUNK), f32),
            vmem((tm, chunks, rows, CHUNK), f32),
            vmem((1, count_rows), f32),
            vmem((space - 1, 1, count_rows), f32),
            vmem((1, count_rows), f32),
            vmem((tm - 1, 1, count_rows), f32),
            vmem((count_rows, CHUNK), f32),
            vmem((chunks, tm - 1, rows, CHUNK), jnp.int16),
            vmem((chunks, tm - 1, 1, CHUNK), f32),
            vmem((chunks, tm - 1, rows, CHUNK), jnp.int16),
            vmem((chunks, tm - 1, 1, CHUNK), f32),
            dma((chunks,)), dma((2,)),
            dma((tm - 1,)), dma((tm - 1,)),
            dma((space - 1,)), dma((space - 1,)),
            dma((tm - 1,)), dma((tm - 1,)),
            dma((stages, chunks)), dma((stages, chunks)), dma((stages, chunks)), dma((stages, chunks)),
        ],
        compiler_params=pltpu.CompilerParams(
            collective_id=0, has_side_effects=True, vmem_limit_bytes=52 * 2**20
        ),
        name="compose",
    )(fields, calendar_day.reshape(days // LANES, LANES), events)
    return pl.pallas_call(
        finish,
        out_shape=jax.ShapeDtypeStruct(shape, f32),
        in_specs=[pl.BlockSpec(memory_space=pltpu.SMEM), pl.BlockSpec(memory_space=vmem)],
        out_specs=pl.BlockSpec(memory_space=pl.ANY),
        scratch_shapes=[dma((lag_count,))],
        compiler_params=pltpu.CompilerParams(vmem_limit_bytes=8 * 2**20),
        name="finish",
    )(lag_offsets, natural)


def solution(mesh):
    return jax.shard_map(
        functools.partial(shards, mesh.shape["tm"], mesh.shape["space"]),
        mesh=mesh,
        in_specs=(P("tm", None, "space"), P("tm"), P(), P()),
        out_specs=P("tm", None, None, "space"),
        check_vma=False,
    )
```

time: 46.9 us -> 35.3 us (0.75)
  Pallas kernels: 44.1 us -> 33.6 us
  other arithmetic: 1.96 us -> 0 us
  local copies, waits for them, and re-layouts: 0.56 us -> 1.4 us
    pallas_call x1, Pallas kernels: 38.8 us -> 32 us  [shards(): pl.pallas_call(functools.partial(compose, tm, space, members, points * sp...]
    pallas_call x2 -> x1, Pallas kernels: 5.28 us -> 1.63 us  [shards(): pl.pallas_call(finish, out_shape=jax.ShapeDtypeStruct(shape, f32), in_spe...]
    unnamed x2 -> x6, local copies, waits for them, and re-layouts: 0.01 us -> 1.4 us
    mul x2 -> x0, other arithmetic: 1.39 us -> none  [the longest x1 0.7 us: shards(): places = 2 * (events - lax.axis_index('tm') * days).T]
    convert_element_type x2 -> x0, other arithmetic: 0.56 us -> none  [the longest x1 0.55 us: regressor_rows(): return rows.astype(jnp.bfloat16)]
where the time goes in v1:
time: 35.3 us; the launch traced here: 35 us
  Pallas kernels  33.6 us (95%)
  local copies, waits for them, and re-layouts  1.4 us (4%)
    pallas_call x1, Pallas kernels, shards(): pl.pallas_call(functools.partial(compose, tm, space, members, points * sp...  32 us
    pallas_call x1, Pallas kernels, shards(): pl.pallas_call(finish, out_shape=jax.ShapeDtypeStruct(shape, f32), in_spe...  1.63 us
    unnamed x6, local copies, waits for them, and re-layouts  1.4 us

profile of v1, /device:TPU:0, one launch (start us, length us, event | category | flops | bytes accessed | tf_op | source)
XLA Modules:
  0.0 35.0 jit_solution(4383604509864129483)
XLA Ops:
  0.0 0.0 copy-start.2
  0.0 0.0 copy-start
  0.0 0.7 %copy-done = s32[16,96]{1,0:T(8,128)S(1)} copy-done((s32[16,96]{1,0:T(8,128)S(1)}, s32[16,96]{1,0:T(8,128)}, u32[]{:S(2)}) %copy-start) | copy-done | bytes 6168
  0.7 0.0 copy-start.1
  0.7 0.7 %copy-done.1 = s32[1024]{0:T(1024)S(1)} copy-done((s32[1024]{0:T(1024)S(1)}, s32[1024]{0:T(1024)}, u32[]{:S(2)}) %copy-start.1) | copy-done | bytes 4120
  1.4 32.0 %compose.1.natural = f32[4,16,2,2048]{3,2,1,0:T(2,128)S(1)} custom-call(bf16[1024,2,2048]{2,1,0:T(2,128)(2,1)} %fields.1, s32[8,128]{1,0:T(8,128)S(1)} %bitcast.1, s32[16,96]{1,0:T(8,128)S(1)} %copy-done), custom_call_target="tpu_custom_call" | custom-call | tf_op jit(solution)/shard_map/compose/pallas_call | solution.py:347
  33.4 0.0 copy-done.2
  33.4 1.6 %finish.1 = f32[4,16,2,2048]{3,2,1,0:T(2,128)} custom-call(s32[16]{0:T(128)S(1)} %copy-done.2, f32[4,16,2,2048]{3,2,1,0:T(2,128)S(1)} %compose.1.natural), custom_call_target="tpu_custom_call" | custom-call | tf_op jit(solution)/shard_map/finish/pallas_call | solution.py:384
Async XLA Ops:
  0.0 33.4 %copy-start.2 = (s32[16]{0:T(128)S(1)}, s32[16]{0:T(128)}, u32[]{:S(2)}) copy-start(s32[16]{0:T(128)} %lags_ref.1) | copy-start | bytes 196
  0.0 0.7 %copy-start = (s32[16,96]{1,0:T(8,128)S(1)}, s32[16,96]{1,0:T(8,128)}, u32[]{:S(2)}) copy-start(s32[16,96]{1,0:T(8,128)} %events.1) | copy-start | bytes 18436
  0.7 0.7 %copy-start.1 = (s32[1024]{0:T(1024)S(1)}, s32[1024]{0:T(1024)}, u32[]{:S(2)}) copy-start(s32[1024]{0:T(1024)} %param.5) | copy-start | bytes 12292

commit v2 on v1

--- a/solution.py
+++ b/solution.py
@@ -53,7 +53,7 @@
 
 def count_weights(places, weights_ref, depth):
     types, members = places.shape
-    shifts = (weights_ref.shape[0] - 32) // types
+    lag_count = (weights_ref.shape[0] - 32) // (2 * types)
     tiles = (depth + PAD) // LANES
     upper = lax.shift_right_arithmetic(places, 7)
     lower = lax.bitwise_and(places, LANES - 1)
@@ -64,10 +64,12 @@
         in_lane = ones_where(lower[kind : kind + 1, :] == lane_lines)
         histogram = lax.dot_general(in_tile, in_lane, NT, preferred_element_type=jnp.float32)
         wide = jnp.concatenate(
-            [jnp.broadcast_to(histogram[tile : tile + 1, :], (shifts, LANES)) for tile in range(tiles)], axis=1
+            [jnp.broadcast_to(histogram[tile : tile + 1, :], (lag_count, LANES)) for tile in range(tiles)], axis=1
         )
-        rolled = pltpu.roll(wide, 0, 1, stride=1, stride_axis=0)
-        weights_ref[kind * shifts : (kind + 1) * shifts, :] = rolled[:, PAD:].astype(jnp.bfloat16)
+        for variable in range(2):
+            rolled = pltpu.roll(wide, variable, 1, stride=2, stride_axis=0)
+            start = (2 * kind + variable) * lag_count
+            weights_ref[start : start + lag_count, :] = rolled[:, PAD:].astype(jnp.bfloat16)
 
 
 def regressors(calendar, weights_ref):
@@ -103,12 +105,12 @@
     return (spread[0] + spread[1]).astype(jnp.bfloat16)
 
 
-def solve(system, count_rows):
+def solve(system, sides_width):
     lines = lax.broadcasted_iota(jnp.int32, (16, LANES), 0)
     columns = [
-        jnp.broadcast_to(system[:, count_rows + k : count_rows + k + 1], (16, LANES)) for k in range(TERMS)
+        jnp.broadcast_to(system[:, sides_width + k : sides_width + k + 1], (16, LANES)) for k in range(TERMS)
     ]
-    sides = [system[:, start : start + LANES] for start in range(0, count_rows, LANES)]
+    sides = [system[:, start : start + LANES] for start in range(0, sides_width, LANES)]
     for k in range(TERMS):
         column = columns[k]
         inverse = 1.0 / column[k : k + 1, :]
@@ -124,8 +126,8 @@
 
 def compose(
     tm, space, members, all_points,
-    fields, calendar, events, out_ref,
-    xs, calendar_ref, events_ref, weights_ref, normal_ref, normals, left, raws, whole, spatial, parts,
+    fields, calendar, events, lags, out_ref,
+    xs, calendar_ref, events_ref, lags_ref, weights_ref, normal_ref, normals, left, raws, whole, spatial, parts, ordered,
     sums, got_sums, totals, got_totals, means, codes, scales, got_codes, got_scales,
     x_sems, in_sems, n_send, n_recv, m_send, m_recv, t_send, t_recv, c_send, c_recv, s_send, s_recv,
 ):
@@ -133,6 +135,9 @@
     depth = weights_ref.shape[1]
     count_rows = weights_ref.shape[0] - 32
     rows = count_rows // tm
+    types = events_ref.shape[0]
+    lag_count = lags_ref.shape[0]
+    maps = types * lag_count
     me = lax.axis_index("tm")
     here = lax.axis_index("space")
     stages = tm.bit_length() - 1
@@ -149,14 +154,20 @@
         pl.semaphore_signal(barrier, inc=1, device_id={"space": lax.rem(here + i, space)})
     load_events = pltpu.make_async_copy(events, events_ref, in_sems.at[0])
     load_calendar = pltpu.make_async_copy(calendar, calendar_ref, in_sems.at[1])
+    load_lags = pltpu.make_async_copy(lags, lags_ref, in_sems.at[2])
     load_events.start()
     load_calendar.start()
+    load_lags.start()
     lax.fori_loop(0, chunks, lambda c, _: (load(c).start(), 0)[1], 0)
 
     def send_normal(i):
-        return pltpu.make_async_remote_copy(
-            normal_ref, normals.at[i - 1], n_send.at[i - 1], n_recv.at[i - 1], device_id={"tm": lax.rem(me + i, tm)}
-        )
+        return [
+            pltpu.make_async_remote_copy(
+                normal_ref.at[lines], normals.at[i - 1, lines], n_send.at[part, i - 1], n_recv.at[part, i - 1],
+                device_id={"tm": lax.rem(me + i, tm)},
+            )
+            for part, lines in enumerate((pl.ds(0, 8), pl.ds(8, 8)))
+        ]
 
     def send_sums(i):
         return pltpu.make_async_remote_copy(
@@ -199,11 +210,16 @@
     count_weights(2 * (events_ref[...] - me * days) + PAD, weights_ref, depth)
     load_calendar.wait()
     design = regressors(calendar_ref[...], weights_ref)
-    normal_ref[...] = lax.dot_general(design, weights_ref[...], NT, preferred_element_type=jnp.float32)
+    first = weights_ref[:count_rows, :].reshape(types, 2 * lag_count, depth)[:, :lag_count, :].reshape(maps, depth)
+    grams = weights_ref[count_rows : count_rows + 16, :]
+    normal_ref[...] = jnp.concatenate(
+        [lax.dot_general(design, side, NT, preferred_element_type=jnp.float32) for side in (first, grams)], axis=1
+    )
 
     pl.semaphore_wait(barrier, tm + space - 2)
     for i in range(1, tm):
-        send_normal(i).start()
+        for copy in send_normal(i):
+            copy.start()
 
     def multiply(c, carry):
         load(c).wait()
@@ -215,11 +231,10 @@
 
     system = normal_ref[...]
     for i in range(1, tm):
-        send_normal(i).wait()
+        for copy in send_normal(i):
+            copy.wait()
         system = system + normals[i - 1]
-    fit = solve(system, count_rows)
-    odd = lax.broadcasted_iota(jnp.int32, fit.shape, 1) % 2
-    fit = jnp.concatenate([jnp.where(odd == 0, fit, 0.0), jnp.where(odd == 1, fit, 0.0)], axis=0)
+    fit = solve(system, maps)
     high, middle, low = [piece.astype(jnp.float32) for piece in split3(fit)]
     left[...] = jnp.transpose(jnp.concatenate([high, high, high, middle, middle, low], axis=0)).astype(jnp.bfloat16)
     spatial[...] = jnp.zeros_like(spatial)
@@ -249,9 +264,15 @@
             parts[apart - bit, c] += decode(got_codes[c, place], got_scales[c, place])
 
     def anomalies(c, turn):
-        p_high, p_middle, p_low = split3(raws[c, count_rows:, :])
-        right = jnp.concatenate([p_high, p_middle, p_low, p_high, p_middle, p_high], axis=0)
-        whole[...] = raws[c, :count_rows, :] - jnp.dot(left[...], right, preferred_element_type=jnp.float32)
+        seasonal = []
+        for variable in range(2):
+            start = count_rows + 16 * variable
+            p_high, p_middle, p_low = split3(raws[c, start : start + 16, :])
+            right = jnp.concatenate([p_high, p_middle, p_low, p_high, p_middle, p_high], axis=0)
+            product = jnp.dot(left[...], right, preferred_element_type=jnp.float32)
+            seasonal.append(product.reshape(types, 1, lag_count, CHUNK))
+        seasonal = jnp.concatenate(seasonal, axis=1).reshape(count_rows, CHUNK)
+        whole[...] = raws[c, :count_rows, :] - seasonal
         for apart in range(tm):
             parts[apart, c] = whole[pl.ds(pl.multiple_of(flip(me, apart) * rows, rows), rows), :]
         post(c, turn, 0)
@@ -305,11 +326,20 @@
         TN, precision=lax.Precision.HIGHEST, preferred_element_type=jnp.float32,
     )
 
+    load_lags.wait()
+
     def gather(c, turn):
         collect(c, turn, stages - 1)
         mean = means[pl.ds(pl.multiple_of(me * rows, rows), rows), :]
         value = parts[0, c] * (1.0 / members) - mean
-        out_ref[:, :, :, pl.ds(pl.multiple_of(c * CHUNK, CHUNK), CHUNK)] = value.reshape(out_ref.shape[:3] + (CHUNK,))
+        ordered[...] = value
+        columns = pl.ds(pl.multiple_of(c * CHUNK, CHUNK), CHUNK)
+        for lag in range(lag_count):
+            shift = lags_ref[lag]
+            for kind in range(types // tm):
+                for variable in range(2):
+                    line = pl.ds((2 * kind + variable) * lag_count + shift, 1)
+                    out_ref[kind, lag, variable : variable + 1, columns] = ordered[line, :]
 
     grouped(gather, 0, chunks)
 
@@ -319,16 +349,6 @@
                 copy.wait_send()
 
     grouped(sent, 0, chunks)
-
-
-def finish(lags_ref, natural, out, sems):
-    def copy(lag):
-        return pltpu.make_async_copy(natural.at[:, lags_ref[lag]], out.at[:, lag], sems.at[lag])
-
-    for lag in range(out.shape[1]):
-        copy(lag).start()
-    for lag in range(out.shape[1]):
-        copy(lag).wait()
 
 
 def shards(tm, space, fields, calendar_day, events, lag_offsets):
@@ -344,23 +364,29 @@
     vmem = pltpu.VMEM
     f32, bf16 = jnp.float32, jnp.bfloat16
     shape = (types // tm, lag_count, variables, points)
-    natural = pl.pallas_call(
+    in_hbm = [
+        pltpu.with_memory_space_constraint(value, pltpu.HBM)
+        for value in (calendar_day.reshape(days // LANES, LANES), events, lag_offsets)
+    ]
+    return pl.pallas_call(
         functools.partial(compose, tm, space, members, points * space),
         out_shape=jax.ShapeDtypeStruct(shape, f32),
-        in_specs=[pl.BlockSpec(memory_space=pltpu.HBM)] * 3,
+        in_specs=[pl.BlockSpec(memory_space=pltpu.HBM)] * 4,
         out_specs=pl.BlockSpec(memory_space=vmem),
         scratch_shapes=[
             vmem((chunks, days, variables, CHUNK), bf16),
             vmem((days // LANES, LANES), jnp.int32),
             vmem((types, members), jnp.int32),
+            pltpu.SMEM((lag_count,), jnp.int32),
             vmem((count_rows + 32, depth), bf16),
-            vmem((16, count_rows + 32), f32),
-            vmem((tm - 1, 16, count_rows + 32), f32),
-            vmem((count_rows, 192), bf16),
+            vmem((16, types * lag_count + 16), f32),
+            vmem((tm - 1, 16, types * lag_count + 16), f32),
+            vmem((types * lag_count, 96), bf16),
             vmem((chunks, count_rows + 32, CHUNK), f32),
             vmem((count_rows, CHUNK), f32),
             vmem((count_rows, CHUNK), f32),
             vmem((tm, chunks, rows, CHUNK), f32),
+            vmem((rows, CHUNK), f32),
             vmem((1, count_rows), f32),
             vmem((space - 1, 1, count_rows), f32),
             vmem((1, count_rows), f32),
@@ -370,8 +396,8 @@
             vmem((chunks, tm - 1, 1, CHUNK), f32),
             vmem((chunks, tm - 1, rows, CHUNK), jnp.int16),
             vmem((chunks, tm - 1, 1, CHUNK), f32),
-            dma((chunks,)), dma((2,)),
-            dma((tm - 1,)), dma((tm - 1,)),
+            dma((chunks,)), dma((3,)),
+            dma((2, tm - 1)), dma((2, tm - 1)),
             dma((space - 1,)), dma((space - 1,)),
             dma((tm - 1,)), dma((tm - 1,)),
             dma((stages, chunks)), dma((stages, chunks)), dma((stages, chunks)), dma((stages, chunks)),
@@ -380,16 +406,7 @@
             collective_id=0, has_side_effects=True, vmem_limit_bytes=52 * 2**20
         ),
         name="compose",
-    )(fields, calendar_day.reshape(days // LANES, LANES), events)
-    return pl.pallas_call(
-        finish,
-        out_shape=jax.ShapeDtypeStruct(shape, f32),
-        in_specs=[pl.BlockSpec(memory_space=pltpu.SMEM), pl.BlockSpec(memory_space=vmem)],
-        out_specs=pl.BlockSpec(memory_space=pl.ANY),
-        scratch_shapes=[dma((lag_count,))],
-        compiler_params=pltpu.CompilerParams(vmem_limit_bytes=8 * 2**20),
-        name="finish",
-    )(lag_offsets, natural)
+    )(fields, *in_hbm)
 
 
 def solution(mesh):

time: 35.3 us -> 33 us (0.935)
  Pallas kernels: 33.6 us -> 31.8 us
  local copies, waits for them, and re-layouts: 1.4 us -> 0.97 us
    pallas_call x1 -> x0, Pallas kernels: 1.63 us -> none  [shards(): pl.pallas_call(finish, out_shape=jax.ShapeDtypeStruct(shape, f32), in_spe...]
    unnamed x6 -> x1, local copies, waits for them, and re-layouts: 1.4 us -> 0.97 us
where the time goes in v2:
time: 33 us; the launch traced here: 32.8 us
  Pallas kernels  31.8 us (96%)
  local copies, waits for them, and re-layouts  0.97 us (3%)
    pallas_call x1, Pallas kernels, shards(): pl.pallas_call(functools.partial(compose, tm, space, members, points * sp...  31.8 us
    unnamed x1, local copies, waits for them, and re-layouts  0.97 us

profile of v2, /device:TPU:0, one launch (start us, length us, event | category | flops | bytes accessed | tf_op | source)
XLA Modules:
  0.0 32.8 jit_solution(16283523412205099467)
XLA Ops:
  0.0 31.8 %compose.1 = f32[4,16,2,2048]{3,2,1,0:T(2,128)S(1)} custom-call(bf16[1024,2,2048]{2,1,0:T(2,128)(2,1)} %fields.1, s32[8,128]{1,0:T(8,128)} %bitcast.1, s32[16,96]{1,0:T(8,128)} %events.1, s32[16]{0:T(128)} %lags.1), custom_call_target="tpu_custom_call" | custom-call | tf_op jit(solution)/shard_map/compose/pallas_call | solution.py:371
  31.8 1.0 %copy.6 = f32[4,16,2,2048]{3,2,1,0:T(2,128)} copy(f32[4,16,2,2048]{3,2,1,0:T(2,128)S(1)} %compose.1) | data formatting | bytes 2097152

commit v3 on v2

--- a/solution.py
+++ b/solution.py
@@ -13,6 +13,7 @@
 LANES = 128
 PAD = 128
 CHUNK = 256
+CORES = 2
 AHEAD = 4
 NN = (((1,), (0,)), ((), ()))
 NT = (((1,), (1,)), ((), ()))
@@ -129,7 +130,7 @@
     fields, calendar, events, lags, out_ref,
     xs, calendar_ref, events_ref, lags_ref, weights_ref, normal_ref, normals, left, raws, whole, spatial, parts, ordered,
     sums, got_sums, totals, got_totals, means, codes, scales, got_codes, got_scales,
-    x_sems, in_sems, n_send, n_recv, m_send, m_recv, t_send, t_recv, c_send, c_recv, s_send, s_recv,
+    ready, x_sems, in_sems, n_send, n_recv, m_send, m_recv, t_send, t_recv, c_send, c_recv, s_send, s_recv,
 ):
     chunks, days = xs.shape[0], xs.shape[1]
     depth = weights_ref.shape[1]
@@ -150,8 +151,28 @@
     barrier = pltpu.get_barrier_semaphore()
     for i in range(1, tm):
         pl.semaphore_signal(barrier, inc=1, device_id={"tm": lax.rem(me + i, tm)})
-    for i in range(1, space):
-        pl.semaphore_signal(barrier, inc=1, device_id={"space": lax.rem(here + i, space)})
+    chip, side, line = lax.div(here, CORES), lax.rem(here, CORES), space // CORES
+
+    def greet(place, core):
+        pl.semaphore_signal(barrier, inc=1, device_id={"space": place * CORES + core})
+
+    def inform(way, place):
+        pl.semaphore_signal(ready.at[way], inc=1, device_id={"space": place * CORES + side})
+
+    for i in range(1, CORES):
+        greet(chip, lax.rem(side + i, CORES))
+
+    @pl.when(chip > 0)
+    def _():
+        for core in range(CORES):
+            greet(chip - 1, core)
+
+    @pl.when(chip < line - 1)
+    def _():
+        for core in range(CORES):
+            greet(chip + 1, core)
+
+    greeted = lax.min(chip, 1) + lax.min(line - 1 - chip, 1)
     load_events = pltpu.make_async_copy(events, events_ref, in_sems.at[0])
     load_calendar = pltpu.make_async_copy(calendar, calendar_ref, in_sems.at[1])
     load_lags = pltpu.make_async_copy(lags, lags_ref, in_sems.at[2])
@@ -216,7 +237,10 @@
         [lax.dot_general(design, side, NT, preferred_element_type=jnp.float32) for side in (first, grams)], axis=1
     )
 
-    pl.semaphore_wait(barrier, tm + space - 2)
+    pl.semaphore_wait(barrier, tm - 1 + CORES - 1 + CORES * greeted)
+    if line > 2:
+        pl.when(chip == 1)(lambda: inform(0, chip + 1))
+        pl.when(chip == line - 2)(lambda: inform(1, chip - 1))
     for i in range(1, tm):
         for copy in send_normal(i):
             copy.start()
@@ -234,6 +258,18 @@
         for copy in send_normal(i):
             copy.wait()
         system = system + normals[i - 1]
+    if line > 3:
+
+        @pl.when(jnp.logical_and(chip >= 2, chip < line - 1))
+        def _():
+            pl.semaphore_wait(ready.at[0], 1)
+            inform(0, chip + 1)
+
+        @pl.when(jnp.logical_and(chip <= line - 3, chip > 0))
+        def _():
+            pl.semaphore_wait(ready.at[1], 1)
+            inform(1, chip - 1)
+
     fit = solve(system, maps)
     high, middle, low = [piece.astype(jnp.float32) for piece in split3(fit)]
     left[...] = jnp.transpose(jnp.concatenate([high, high, high, middle, middle, low], axis=0)).astype(jnp.bfloat16)
@@ -290,6 +326,9 @@
     for piece in split3(spatial[...]):
         total = total + lax.dot_general(ones, piece, NT, preferred_element_type=jnp.float32)
     sums[...] = total[0:1, :]
+    if line > 2:
+        pl.when(chip == line - 1)(lambda: pl.semaphore_wait(ready.at[0], 1))
+        pl.when(chip == 0)(lambda: pl.semaphore_wait(ready.at[1], 1))
     for i in range(1, space):
         send_sums(i).start()
 
@@ -396,6 +435,7 @@
             vmem((chunks, tm - 1, 1, CHUNK), f32),
             vmem((chunks, tm - 1, rows, CHUNK), jnp.int16),
             vmem((chunks, tm - 1, 1, CHUNK), f32),
+            pltpu.SemaphoreType.REGULAR((2,)),
             dma((chunks,)), dma((3,)),
             dma((2, tm - 1)), dma((2, tm - 1)),
             dma((space - 1,)), dma((space - 1,)),

time: 33 us -> 31.3 us (0.948)
  Pallas kernels: 31.8 us -> 30.1 us
    pallas_call x1, Pallas kernels: 31.8 us -> 30.1 us  [shards(): pl.pallas_call(functools.partial(compose, tm, space, members, points * sp...]
where the time goes in v3:
time: 31.3 us; the launch traced here: 31.1 us
  Pallas kernels  30.1 us (96%)
  local copies, waits for them, and re-layouts  0.97 us (3%)
    pallas_call x1, Pallas kernels, shards(): pl.pallas_call(functools.partial(compose, tm, space, members, points * sp...  30.1 us
    unnamed x1, local copies, waits for them, and re-layouts  0.97 us

profile of v3, /device:TPU:0, one launch (start us, length us, event | category | flops | bytes accessed | tf_op | source)
XLA Modules:
  0.0 31.1 jit_solution(14144521658076043122)
XLA Ops:
  0.0 30.1 %compose.1 = f32[4,16,2,2048]{3,2,1,0:T(2,128)S(1)} custom-call(bf16[1024,2,2048]{2,1,0:T(2,128)(2,1)} %fields.1, s32[8,128]{1,0:T(8,128)} %bitcast.1, s32[16,96]{1,0:T(8,128)} %events.1, s32[16]{0:T(128)} %lags.1), custom_call_target="tpu_custom_call" | custom-call | tf_op jit(solution)/shard_map/compose/pallas_call | solution.py:410
  30.1 1.0 %copy.6 = f32[4,16,2,2048]{3,2,1,0:T(2,128)} copy(f32[4,16,2,2048]{3,2,1,0:T(2,128)S(1)} %compose.1) | data formatting | bytes 2097152

commit v4 on v2

v4 whole, which is shorter than its diff:
```python
import functools

import jax
import jax.numpy as jnp
from jax import lax
from jax.experimental import pallas as pl
from jax.experimental.pallas import tpu as pltpu
from jax.sharding import PartitionSpec as P

HARMONICS = 4
TERMS = 2 * HARMONICS + 1
TWO_PI = 6.283185307179586
LANES = 128
PAD = 128
CHUNK = 256
AHEAD = 2
TURNS = 2
NN = (((1,), (0,)), ((), ()))
NT = (((1,), (1,)), ((), ()))
TN = (((0,), (0,)), ((), ()))


def split3(value):
    high = value.astype(jnp.bfloat16)
    rest = value - high.astype(jnp.float32)
    middle = rest.astype(jnp.bfloat16)
    low = (rest - middle.astype(jnp.float32)).astype(jnp.bfloat16)
    return high, middle, low


def encode(part):
    top = jnp.max(jnp.abs(part), axis=0, keepdims=True)
    factor = jnp.where(top > 0.0, 32767.0 / jnp.where(top > 0.0, top, 1.0), 0.0)
    return jnp.round(part * factor).astype(jnp.int32).astype(jnp.int16), top * (1.0 / 32767.0)


def decode(codes, scale):
    return codes.astype(jnp.int32).astype(jnp.float32) * scale


def flip(index, bits):
    bit = 1
    flipped = index
    while bit <= bits:
        if bits & bit:
            flipped = flipped + bit - 2 * bit * lax.rem(lax.div(index, bit), 2)
        bit *= 2
    return flipped


def ones_where(condition):
    return jnp.where(condition, 1.0, 0.0).astype(jnp.bfloat16)


def histograms(places, tiles):
    members = places.shape[1]
    upper = lax.shift_right_arithmetic(places, 7)
    lower = lax.bitwise_and(places, LANES - 1)
    tile_lines = lax.broadcasted_iota(jnp.int32, (-(-tiles // 8) * 8, members), 0)
    lane_lines = lax.broadcasted_iota(jnp.int32, (LANES, members), 0)
    for kind in range(places.shape[0]):
        in_tile = ones_where(upper[kind : kind + 1, :] == tile_lines)
        in_lane = ones_where(lower[kind : kind + 1, :] == lane_lines)
        yield lax.dot_general(in_tile, in_lane, NT, preferred_element_type=jnp.float32)


def widen(histogram, tiles, lines):
    return jnp.concatenate(
        [jnp.broadcast_to(histogram[tile : tile + 1, :], (lines, LANES)) for tile in range(tiles)], axis=1
    )


def count_weights(places, weights_ref, lag_count):
    tiles = (weights_ref.shape[1] + PAD) // LANES
    for kind, histogram in enumerate(histograms(places, tiles)):
        wide = widen(histogram, tiles, lag_count)
        for variable in range(2):
            rolled = pltpu.roll(wide, variable, 1, stride=2, stride_axis=0)
            start = (2 * kind + variable) * lag_count
            weights_ref[start : start + lag_count, :] = rolled[:, PAD:].astype(jnp.bfloat16)


def count_days(places, counts_ref, lag_count):
    tiles = (counts_ref.shape[1] + PAD) // LANES
    for kind, histogram in enumerate(histograms(places, tiles)):
        rolled = pltpu.roll(widen(histogram, tiles, lag_count), 0, 1, stride=1, stride_axis=0)
        counts_ref[kind * lag_count : (kind + 1) * lag_count, :] = rolled[:, PAD:].astype(jnp.bfloat16)


def regressors(calendar):
    phase = calendar.astype(jnp.float32) * (TWO_PI / 365.25)
    cosines, sines = [jnp.cos(phase)], [jnp.sin(phase)]
    for order in range(2, HARMONICS + 1):
        a, b = order // 2 - 1, order - order // 2 - 1
        cosines.append(cosines[a] * cosines[b] - sines[a] * sines[b])
        sines.append(sines[a] * cosines[b] + cosines[a] * sines[b])
    terms = [jnp.ones_like(phase)]
    for order in range(HARMONICS):
        terms += [cosines[order], sines[order]]
    line = lax.broadcasted_iota(jnp.int32, (16, LANES), 0)
    blocks = []
    for tile in range(calendar.shape[0]):
        block = jnp.zeros((16, LANES), jnp.float32)
        for term, values in enumerate(terms):
            block = jnp.where(line == term, values[tile : tile + 1, :], block)
        blocks.append(block)
    return blocks


def own_regressors(calendar, weights_ref):
    tiles = calendar.shape[0]
    stacked = jnp.concatenate(regressors(calendar), axis=0).astype(jnp.bfloat16)
    day = lax.broadcasted_iota(jnp.int32, (LANES, 2 * LANES), 0)
    place = lax.broadcasted_iota(jnp.int32, (LANES, 2 * LANES), 1)
    start = weights_ref.shape[0] - 32
    for variable in range(2):
        spread = jnp.dot(stacked, ones_where(place == 2 * day + variable), preferred_element_type=jnp.float32)
        lines = jnp.concatenate([spread[16 * tile : 16 * tile + 16, :] for tile in range(tiles)], axis=1)
        weights_ref[start + 16 * variable : start + 16 * variable + 16, :] = lines.astype(jnp.bfloat16)


def solve(system, sides_width):
    lines = lax.broadcasted_iota(jnp.int32, (16, LANES), 0)
    columns = [
        jnp.broadcast_to(system[:, sides_width + k : sides_width + k + 1], (16, LANES)) for k in range(TERMS)
    ]
    sides = [system[:, start : start + LANES] for start in range(0, sides_width, LANES)]
    for k in range(TERMS):
        column = columns[k]
        inverse = 1.0 / column[k : k + 1, :]

        def eliminate(block):
            pivot = block[k : k + 1, :] * inverse
            return jnp.where(lines == k, pivot, block - column * pivot)

        sides = [eliminate(block) for block in sides]
        columns = [eliminate(block) if j > k else block for j, block in enumerate(columns)]
    return jnp.concatenate([jnp.where(lines < TERMS, block, 0.0) for block in sides], axis=1)


def compose(
    tm, space, members, all_points,
    fields, calendar, events, lags, out_ref,
    xs, calendars, events_ref, lags_ref, weights_ref, counts_ref, left, raws, whole, spatial, parts, order,
    sums, got_sums, totals, got_totals, means, codes, scales, got_codes, got_scales,
    ready, x_sems, in_sems, n_send, n_recv, m_send, m_recv, t_send, t_recv, c_send, c_recv, s_send, s_recv,
):
    chunks, days = xs.shape[0], xs.shape[1]
    depth = weights_ref.shape[1]
    count_rows = weights_ref.shape[0] - 32
    rows = count_rows // tm
    types = events_ref.shape[0]
    lag_count = lags_ref.shape[0]
    maps = types * lag_count
    me = lax.axis_index("tm")
    here = lax.axis_index("space")
    stages = tm.bit_length() - 1

    def load(c):
        return pltpu.make_async_copy(
            fields.at[:, :, pl.ds(pl.multiple_of(c * CHUNK, CHUNK), CHUNK)], xs.at[c], x_sems.at[c]
        )

    barrier = pltpu.get_barrier_semaphore()
    for i in range(1, tm):
        pl.semaphore_signal(barrier, inc=1, device_id={"tm": lax.rem(me + i, tm)})

    def greet(place, carry):
        pl.semaphore_signal(barrier, inc=1, device_id={"space": place})
        return carry

    def answer(place, carry):
        pl.semaphore_signal(ready, inc=1, device_id={"space": place})
        return carry

    lax.fori_loop(here + 1, space, greet, 0)
    load_events = pltpu.make_async_copy(events, events_ref, in_sems.at[0])
    tiles = days // LANES
    own = pl.ds(pl.multiple_of(me * tiles, tiles), tiles)
    load_calendar = pltpu.make_async_copy(calendar, calendars.at[own], in_sems.at[1])
    load_lags = pltpu.make_async_copy(lags, lags_ref, in_sems.at[2])
    load_calendar.start()
    load_events.start()
    load_lags.start()
    lax.fori_loop(0, chunks, lambda c, _: (load(c).start(), 0)[1], 0)

    def send_calendar(i):
        return pltpu.make_async_remote_copy(
            calendars.at[own], calendars.at[own], n_send.at[i - 1], n_recv.at[i - 1],
            device_id={"tm": lax.rem(me + i, tm)},
        )

    def send_sums(i):
        return pltpu.make_async_remote_copy(
            sums, got_sums.at[i - 1], m_send.at[i - 1], m_recv.at[i - 1],
            device_id={"space": lax.rem(here + i, space)},
        )

    def send_totals(i):
        return pltpu.make_async_remote_copy(
            totals, got_totals.at[i - 1], t_send.at[i - 1], t_recv.at[i - 1],
            device_id={"tm": lax.rem(me + i, tm)},
        )

    def bits_of(turn):
        return [1 << ((turn * stages // TURNS + stage) % stages) for stage in range(stages)]

    half_rows = rows // TURNS

    def leaving(turn, stage):
        bits = bits_of(turn)
        return [
            apart for apart in range(1, tm)
            if apart & bits[stage] and not any(apart & bit for bit in bits[:stage])
        ]

    def first_slot(stage):
        return tm - (tm >> stage)

    def send_codes(c, turn, stage):
        peer = {"tm": flip(me, bits_of(turn)[stage])}
        slots = pl.ds(first_slot(stage), tm >> (stage + 1))
        return (
            pltpu.make_async_remote_copy(
                codes.at[c, turn, slots], got_codes.at[c, turn, slots],
                c_send.at[stage, turn, c], c_recv.at[stage, turn, c], device_id=peer,
            ),
            pltpu.make_async_remote_copy(
                scales.at[c, turn, slots], got_scales.at[c, turn, slots],
                s_send.at[stage, turn, c], s_recv.at[stage, turn, c], device_id=peer,
            ),
        )

    load_calendar.wait()
    pl.semaphore_wait(barrier, tm - 1 + here)
    for i in range(1, tm):
        send_calendar(i).start()
    lax.fori_loop(0, here, answer, 0)
    load_events.wait()
    count_weights(2 * (events_ref[...] - me * days) + PAD, weights_ref, lag_count)
    count_days(events_ref[...] + PAD, counts_ref, lag_count)
    own_regressors(calendars[own, :], weights_ref)

    def multiply(c):
        load(c).wait()
        raws[c] = jnp.dot(weights_ref[...], xs[c].reshape(depth, CHUNK), preferred_element_type=jnp.float32)

    def each(body, start, stop):
        lax.fori_loop(start, stop, lambda c, _: (body(c), 0)[1], 0)

    each(multiply, 0, AHEAD)

    for i in range(1, tm):
        send_calendar(i).wait()
    design = jnp.concatenate(regressors(calendars[...]), axis=1).astype(jnp.bfloat16)
    system = jnp.concatenate(
        [
            lax.dot_general(design, side, NT, preferred_element_type=jnp.float32)
            for side in (counts_ref[...], design)
        ],
        axis=1,
    )
    fit = solve(system, maps)
    high, middle, low = [piece.astype(jnp.float32) for piece in split3(fit)]
    left[...] = jnp.transpose(jnp.concatenate([high, high, high, middle, middle, low], axis=0)).astype(jnp.bfloat16)
    spatial[...] = jnp.zeros_like(spatial)

    def post(c, stage):
        for turn in range(TURNS):
            lines = slice(turn * half_rows, (turn + 1) * half_rows)
            for slot, apart in enumerate(leaving(turn, stage)):
                place = first_slot(stage) + slot
                codes[c, turn, place], scales[c, turn, place] = encode(parts[apart, c, lines])
            for copy in send_codes(c, turn, stage):
                copy.start()

    def collect(c, stage):
        for turn in range(TURNS):
            bit = bits_of(turn)[stage]
            lines = slice(turn * half_rows, (turn + 1) * half_rows)
            for copy in send_codes(c, turn, stage):
                copy.wait_recv()
            for slot, apart in enumerate(leaving(turn, stage)):
                place = first_slot(stage) + slot
                parts[apart - bit, c, lines] += decode(got_codes[c, turn, place], got_scales[c, turn, place])

    def anomalies(c):
        seasonal = []
        for variable in range(2):
            start = count_rows + 16 * variable
            p_high, p_middle, p_low = split3(raws[c, start : start + 16, :])
            right = jnp.concatenate([p_high, p_middle, p_low, p_high, p_middle, p_high], axis=0)
            product = jnp.dot(left[...], right, preferred_element_type=jnp.float32)
            seasonal.append(product.reshape(types, 1, lag_count, CHUNK))
        seasonal = jnp.concatenate(seasonal, axis=1).reshape(count_rows, CHUNK)
        whole[...] = raws[c, :count_rows, :] - seasonal
        for apart in range(tm):
            parts[apart, c] = whole[pl.ds(pl.multiple_of(flip(me, apart) * rows, rows), rows), :]
        post(c, 0)
        spatial[...] += whole[...]

    def both(c):
        anomalies(c)
        multiply(c + AHEAD)

    each(both, 0, chunks - AHEAD)
    each(anomalies, chunks - AHEAD, chunks)

    ones = jnp.ones((8, CHUNK), jnp.bfloat16)
    total = jnp.zeros((8, count_rows), jnp.float32)
    for piece in split3(spatial[...]):
        total = total + lax.dot_general(ones, piece, NT, preferred_element_type=jnp.float32)
    sums[...] = total[0:1, :]

    @pl.when(here < space - 1)
    def _():
        pl.semaphore_wait(ready, space - 1 - here)

    for i in range(1, space):
        send_sums(i).start()

    load_lags.wait()
    target = lax.broadcasted_iota(jnp.int32, (rows, rows), 0)
    source = lax.broadcasted_iota(jnp.int32, (rows, rows), 1)
    group = 2 * lag_count
    assert group & (group - 1) == 0
    inside = lax.bitwise_and(target, group - 1)
    base = target - inside + lax.bitwise_and(target, 1) * lag_count
    place = lax.shift_right_logical(inside, 1)
    wanted = base
    for lag in range(lag_count):
        wanted = jnp.where(place == lag, base + lags_ref[lag], wanted)
    order[...] = ones_where(source == wanted)

    half = chunks // 2

    def relay(stage):
        def body(c):
            collect(c, stage - 1)
            post(c, stage)

        return body

    def spread_sums():
        total = sums[...]
        for i in range(1, space):
            send_sums(i).wait()
            total = total + got_sums[i - 1]
        totals[...] = total
        for i in range(1, tm):
            send_totals(i).start()

    for stage in range(1, stages):
        each(relay(stage), 0, half)
        if stage == 1:
            spread_sums()
        each(relay(stage), half, chunks)

    total = totals[...]
    for i in range(1, tm):
        send_totals(i).wait()
        total = total + got_totals[i - 1]
    means[...] = lax.dot_general(
        jnp.broadcast_to(total * (1.0 / (8 * members * all_points)), (8, count_rows)), jnp.ones((8, CHUNK), jnp.float32),
        TN, precision=lax.Precision.HIGHEST, preferred_element_type=jnp.float32,
    )


    def gather(c):
        collect(c, stages - 1)
        mean = means[pl.ds(pl.multiple_of(me * rows, rows), rows), :]
        value = parts[0, c] * (1.0 / members) - mean
        placed = sum(jnp.dot(order[...], piece, preferred_element_type=jnp.float32) for piece in split3(value))
        columns = pl.ds(pl.multiple_of(c * CHUNK, CHUNK), CHUNK)
        out_ref[:, :, :, columns] = placed.reshape(out_ref.shape[:3] + (CHUNK,))

    each(gather, 0, chunks)

    def sent(c):
        for turn in range(TURNS):
            for stage in range(stages):
                for copy in send_codes(c, turn, stage):
                    copy.wait_send()

    each(sent, 0, chunks)


def shards(tm, space, fields, calendar_day, events, lag_offsets):
    types, members = events.shape
    lag_count = lag_offsets.shape[0]
    days, variables, points = fields.shape
    depth = variables * days
    count_rows = types * lag_count * variables
    rows = count_rows // tm
    chunks = points // CHUNK
    sent = (chunks, TURNS, tm - 1)
    copies = (tm.bit_length() - 1, TURNS, chunks)
    dma = pltpu.SemaphoreType.DMA
    vmem = pltpu.VMEM
    f32, bf16 = jnp.float32, jnp.bfloat16
    shape = (types // tm, lag_count, variables, points)
    in_hbm = [
        pltpu.with_memory_space_constraint(value, pltpu.HBM)
        for value in (calendar_day.reshape(days // LANES, LANES), events, lag_offsets)
    ]
    return pl.pallas_call(
        functools.partial(compose, tm, space, members, points * space),
        out_shape=jax.ShapeDtypeStruct(shape, f32),
        in_specs=[pl.BlockSpec(memory_space=pltpu.HBM)] * 4,
        out_specs=pl.BlockSpec(memory_space=vmem),
        scratch_shapes=[
            vmem((chunks, days, variables, CHUNK), bf16),
            vmem((tm * days // LANES, LANES), jnp.int32),
            vmem((types, members), jnp.int32),
            pltpu.SMEM((lag_count,), jnp.int32),
            vmem((count_rows + 32, depth), bf16),
            vmem((types * lag_count, tm * days), bf16),
            vmem((types * lag_count, 96), bf16),
            vmem((chunks, count_rows + 32, CHUNK), f32),
            vmem((count_rows, CHUNK), f32),
            vmem((count_rows, CHUNK), f32),
            vmem((tm, chunks, rows, CHUNK), f32),
            vmem((rows, rows), bf16),
            vmem((1, count_rows), f32),
            vmem((space - 1, 1, count_rows), f32),
            vmem((1, count_rows), f32),
            vmem((tm - 1, 1, count_rows), f32),
            vmem((count_rows, CHUNK), f32),
            vmem(sent + (rows // TURNS, CHUNK), jnp.int16),
            vmem(sent + (1, CHUNK), f32),
            vmem(sent + (rows // TURNS, CHUNK), jnp.int16),
            vmem(sent + (1, CHUNK), f32),
            pltpu.SemaphoreType.REGULAR,
            dma((chunks,)), dma((3,)),
            dma((tm - 1,)), dma((tm - 1,)),
            dma((space - 1,)), dma((space - 1,)),
            dma((tm - 1,)), dma((tm - 1,)),
            dma(copies), dma(copies), dma(copies), dma(copies),
        ],
        compiler_params=pltpu.CompilerParams(
            collective_id=0, has_side_effects=True, vmem_limit_bytes=52 * 2**20
        ),
        name="compose",
    )(fields, *in_hbm)


def solution(mesh):
    return jax.shard_map(
        functools.partial(shards, mesh.shape["tm"], mesh.shape["space"]),
        mesh=mesh,
        in_specs=(P("tm", None, "space"), P("tm"), P(), P()),
        out_specs=P("tm", None, None, "space"),
        check_vma=False,
    )
```

time: 33 us -> 30.7 us (0.930)
  Pallas kernels: 31.8 us -> 29.5 us
    pallas_call x1, Pallas kernels: 31.8 us -> 29.5 us  [shards(): pl.pallas_call(functools.partial(compose, tm, space, members, points * sp...]
where the time goes in v4:
time: 30.7 us; the launch traced here: 30.5 us
  Pallas kernels  29.5 us (96%)
  local copies, waits for them, and re-layouts  0.97 us (3%)
    pallas_call x1, Pallas kernels, shards(): pl.pallas_call(functools.partial(compose, tm, space, members, points * sp...  29.5 us
    unnamed x1, local copies, waits for them, and re-layouts  0.97 us

profile of v4, /device:TPU:0, one launch (start us, length us, event | category | flops | bytes accessed | tf_op | source)
XLA Modules:
  0.0 30.5 jit_solution(5341448372047595983)
XLA Ops:
  0.0 29.5 %compose.1 = f32[4,16,2,2048]{3,2,1,0:T(2,128)S(1)} custom-call(bf16[1024,2,2048]{2,1,0:T(2,128)(2,1)} %fields.1, s32[8,128]{1,0:T(8,128)} %bitcast.1, s32[16,96]{1,0:T(8,128)} %events.1, s32[16]{0:T(128)} %lags.1), custom_call_target="tpu_custom_call" | custom-call | tf_op jit(solution)/shard_map/compose/pallas_call | solution.py:406
  29.5 1.0 %copy.6 = f32[4,16,2,2048]{3,2,1,0:T(2,128)} copy(f32[4,16,2,2048]{3,2,1,0:T(2,128)S(1)} %compose.1) | data formatting | bytes 2097152

commit v5 on v4

--- a/solution.py
+++ b/solution.py
@@ -12,8 +12,8 @@
 TWO_PI = 6.283185307179586
 LANES = 128
 PAD = 128
-CHUNK = 256
-AHEAD = 2
+CHUNK = 512
+AHEAD = 1
 TURNS = 2
 NN = (((1,), (0,)), ((), ()))
 NT = (((1,), (1,)), ((), ()))
@@ -332,7 +332,7 @@
         wanted = jnp.where(place == lag, base + lags_ref[lag], wanted)
     order[...] = ones_where(source == wanted)
 
-    half = chunks // 2
+    half = chunks // 4
 
     def relay(stage):
         def body(c):

time: 30.7 us -> 29.7 us (0.967)
  Pallas kernels: 29.5 us -> 28.6 us
    pallas_call x1, Pallas kernels: 29.5 us -> 28.6 us  [shards(): pl.pallas_call(functools.partial(compose, tm, space, members, points * sp...]
where the time goes in v5:
time: 29.7 us; the launch traced here: 29.6 us
  Pallas kernels  28.6 us (96%)
  local copies, waits for them, and re-layouts  0.97 us (3%)
    pallas_call x1, Pallas kernels, shards(): pl.pallas_call(functools.partial(compose, tm, space, members, points * sp...  28.6 us
    unnamed x1, local copies, waits for them, and re-layouts  0.97 us

profile of v5, /device:TPU:0, one launch (start us, length us, event | category | flops | bytes accessed | tf_op | source)
XLA Modules:
  0.0 29.6 jit_solution(10964833553716635061)
XLA Ops:
  0.0 28.6 %compose.1 = f32[4,16,2,2048]{3,2,1,0:T(2,128)S(1)} custom-call(bf16[1024,2,2048]{2,1,0:T(2,128)(2,1)} %fields.1, s32[8,128]{1,0:T(8,128)} %bitcast.1, s32[16,96]{1,0:T(8,128)} %events.1, s32[16]{0:T(128)} %lags.1), custom_call_target="tpu_custom_call" | custom-call | tf_op jit(solution)/shard_map/compose/pallas_call | solution.py:406
  28.6 1.0 %copy.6 = f32[4,16,2,2048]{3,2,1,0:T(2,128)} copy(f32[4,16,2,2048]{3,2,1,0:T(2,128)S(1)} %compose.1) | data formatting | bytes 2097152

commit v6 on v5

--- a/solution.py
+++ b/solution.py
@@ -265,8 +265,8 @@
     left[...] = jnp.transpose(jnp.concatenate([high, high, high, middle, middle, low], axis=0)).astype(jnp.bfloat16)
     spatial[...] = jnp.zeros_like(spatial)
 
-    def post(c, stage):
-        for turn in range(TURNS):
+    def post(c, stage, turns=range(TURNS)):
+        for turn in turns:
             lines = slice(turn * half_rows, (turn + 1) * half_rows)
             for slot, apart in enumerate(leaving(turn, stage)):
                 place = first_slot(stage) + slot
@@ -274,8 +274,8 @@
             for copy in send_codes(c, turn, stage):
                 copy.start()
 
-    def collect(c, stage):
-        for turn in range(TURNS):
+    def collect(c, stage, turns=range(TURNS)):
+        for turn in turns:
             bit = bits_of(turn)[stage]
             lines = slice(turn * half_rows, (turn + 1) * half_rows)
             for copy in send_codes(c, turn, stage):
@@ -336,8 +336,9 @@
 
     def relay(stage):
         def body(c):
-            collect(c, stage - 1)
-            post(c, stage)
+            for turn in range(TURNS):
+                collect(c, stage - 1, [turn])
+                post(c, stage, [turn])
 
         return body
 
@@ -361,7 +362,7 @@
         send_totals(i).wait()
         total = total + got_totals[i - 1]
     means[...] = lax.dot_general(
-        jnp.broadcast_to(total * (1.0 / (8 * members * all_points)), (8, count_rows)), jnp.ones((8, CHUNK), jnp.float32),
+        jnp.broadcast_to(total * (1.0 / (8 * members * all_points)), (8, count_rows)), jnp.ones((8, LANES), jnp.float32),
         TN, precision=lax.Precision.HIGHEST, preferred_element_type=jnp.float32,
     )
 
@@ -369,6 +370,7 @@
     def gather(c):
         collect(c, stages - 1)
         mean = means[pl.ds(pl.multiple_of(me * rows, rows), rows), :]
+        mean = jnp.concatenate([mean] * (CHUNK // LANES), axis=1)
         value = parts[0, c] * (1.0 / members) - mean
         placed = sum(jnp.dot(order[...], piece, preferred_element_type=jnp.float32) for piece in split3(value))
         columns = pl.ds(pl.multiple_of(c * CHUNK, CHUNK), CHUNK)
@@ -425,7 +427,7 @@
             vmem((space - 1, 1, count_rows), f32),
             vmem((1, count_rows), f32),
             vmem((tm - 1, 1, count_rows), f32),
-            vmem((count_rows, CHUNK), f32),
+            vmem((count_rows, LANES), f32),
             vmem(sent + (rows // TURNS, CHUNK), jnp.int16),
             vmem(sent + (1, CHUNK), f32),
             vmem(sent + (rows // TURNS, CHUNK), jnp.int16),

time: 29.7 us -> 29.7 us (level)
  no operation moved by 1% of the time
where the time goes in v6:
time: 29.7 us; the launch traced here: 29.6 us
  Pallas kernels  28.6 us (96%)
  local copies, waits for them, and re-layouts  0.97 us (3%)
    pallas_call x1, Pallas kernels, shards(): pl.pallas_call(functools.partial(compose, tm, space, members, points * sp...  28.6 us
    unnamed x1, local copies, waits for them, and re-layouts  0.97 us

profile of v6, /device:TPU:0, one launch (start us, length us, event | category | flops | bytes accessed | tf_op | source)
XLA Modules:
  0.0 29.6 jit_solution(15937821330067919042)
XLA Ops:
  0.0 28.6 %compose.1 = f32[4,16,2,2048]{3,2,1,0:T(2,128)S(1)} custom-call(bf16[1024,2,2048]{2,1,0:T(2,128)(2,1)} %fields.1, s32[8,128]{1,0:T(8,128)} %bitcast.1, s32[16,96]{1,0:T(8,128)} %events.1, s32[16]{0:T(128)} %lags.1), custom_call_target="tpu_custom_call" | custom-call | tf_op jit(solution)/shard_map/compose/pallas_call | solution.py:408
  28.6 1.0 %copy.6 = f32[4,16,2,2048]{3,2,1,0:T(2,128)} copy(f32[4,16,2,2048]{3,2,1,0:T(2,128)S(1)} %compose.1) | data formatting | bytes 2097152

commit v7 on v5

--- a/solution.py
+++ b/solution.py
@@ -367,9 +367,15 @@
 
 
     def gather(c):
-        collect(c, stages - 1)
+        pieces = []
+        for turn in range(TURNS):
+            for copy in send_codes(c, turn, stages - 1):
+                copy.wait_recv()
+            lines = slice(turn * half_rows, (turn + 1) * half_rows)
+            place = first_slot(stages - 1)
+            pieces.append(parts[0, c, lines] + decode(got_codes[c, turn, place], got_scales[c, turn, place]))
         mean = means[pl.ds(pl.multiple_of(me * rows, rows), rows), :]
-        value = parts[0, c] * (1.0 / members) - mean
+        value = jnp.concatenate(pieces, axis=0) * (1.0 / members) - mean
         placed = sum(jnp.dot(order[...], piece, preferred_element_type=jnp.float32) for piece in split3(value))
         columns = pl.ds(pl.multiple_of(c * CHUNK, CHUNK), CHUNK)
         out_ref[:, :, :, columns] = placed.reshape(out_ref.shape[:3] + (CHUNK,))

time: 29.7 us -> 29.7 us (level)
  no operation moved by 1% of the time
where the time goes in v7:
time: 29.7 us; the launch traced here: 29.6 us
  Pallas kernels  28.6 us (96%)
  local copies, waits for them, and re-layouts  0.97 us (3%)
    pallas_call x1, Pallas kernels, shards(): pl.pallas_call(functools.partial(compose, tm, space, members, points * sp...  28.6 us
    unnamed x1, local copies, waits for them, and re-layouts  0.97 us

profile of v7, /device:TPU:0, one launch (start us, length us, event | category | flops | bytes accessed | tf_op | source)
XLA Modules:
  0.0 29.6 jit_solution(18374086454018579411)
XLA Ops:
  0.0 28.6 %compose.1 = f32[4,16,2,2048]{3,2,1,0:T(2,128)S(1)} custom-call(bf16[1024,2,2048]{2,1,0:T(2,128)(2,1)} %fields.1, s32[8,128]{1,0:T(8,128)} %bitcast.1, s32[16,96]{1,0:T(8,128)} %events.1, s32[16]{0:T(128)} %lags.1), custom_call_target="tpu_custom_call" | custom-call | tf_op jit(solution)/shard_map/compose/pallas_call | solution.py:412
  28.6 1.0 %copy.6 = f32[4,16,2,2048]{3,2,1,0:T(2,128)} copy(f32[4,16,2,2048]{3,2,1,0:T(2,128)S(1)} %compose.1) | data formatting | bytes 2097152
